TPU v7x, 32 devices: a whole 2x2x4 slice. The times are simulated.
32 devices in a mesh: chan: 8 (over z, y), beam: 4 (over x, core).
Axes of the slice: x: 2, y: 2, z: 4, core: 2. Of those that a mesh axis runs over, the one named last changes fastest.
Arguments:
- signals: bfloat16 [2048, 8192], P('chan', 'beam'), may hold values from -6 to 6
- weights: bfloat16 [3, 2, 512, 2048], P(None, None, 'beam', 'chan'), may hold values from -0.125 to 0.125
- bin_group: int32 [256], replicated, may hold values from 0 to 2
Outputs:
- formed: float32 [256, 2, 512], P('chan', None, 'beam')
All inputs are finite; a program needn't handle non-finite values.
Results may differ from a plain program's by a relative error of at most 0.0042.
Values may be sent and summed in bfloat16 or wider, within the bound.
A program may use at most 64 MiB of HBM per device.

v0:
```python
import math

import jax
import jax.numpy as jnp
from jax import lax
from jax.sharding import PartitionSpec as P


def complex_terms(weight_block, spec_block, onehot):
    selected = onehot[:, :, None, None] * spec_block[:, None, :, :]
    products = jnp.einsum(
        "gpbc,fgqc->fpqb", weight_block, selected, preferred_element_type=jnp.float32
    )
    real_part = products[:, 0, 0] - products[:, 1, 1]
    imag_part = products[:, 0, 1] + products[:, 1, 0]
    return jnp.stack([real_part, imag_part], 1)


def transform(samples, first_sample, span, total_samples, bin_count):
    block = 512
    frequency = jnp.arange(1, bin_count + 1, dtype=jnp.int32)

    def add_block(step, running):
        start = step * block
        piece = lax.dynamic_slice_in_dim(samples, start, block, 1)
        sample_index = first_sample + start + jnp.arange(block, dtype=jnp.int32)
        phases = frequency[:, None] * sample_index[None, :] % total_samples
        angles = 2.0 * math.pi / total_samples * phases.astype(jnp.float32)
        twiddle = jnp.stack([jnp.cos(angles), -jnp.sin(angles)], 1).astype(jnp.bfloat16)
        return running + lax.dot_general(
            twiddle, piece, (((2,), (1,)), ((), ())), preferred_element_type=jnp.float32
        )

    empty = jnp.zeros((bin_count, 2, samples.shape[0]), jnp.float32)
    return lax.fori_loop(0, span // block, add_block, empty)


def shards(signals, weights, bin_group):
    samples_dev = signals.shape[1]
    total_samples = samples_dev * lax.axis_size("beam")
    bin_count = bin_group.shape[0]
    set_count = weights.shape[0]
    scale = 1.0 / math.sqrt(total_samples)
    full_time = lax.all_to_all(signals, "beam", split_axis=0, concat_axis=1, tiled=True)
    partial_value = transform(full_time, 0, total_samples, total_samples, bin_count)
    own_spec = (partial_value * scale).astype(jnp.bfloat16)
    spectrum = lax.all_gather(own_spec, "beam", axis=2, tiled=True)
    bin_dev = bin_count // lax.axis_size("chan")
    set_ids = jnp.arange(set_count, dtype=jnp.int32)
    local_spec = lax.all_to_all(spectrum, "chan", split_axis=0, concat_axis=2, tiled=True)
    local_sets = lax.dynamic_slice_in_dim(bin_group, lax.axis_index("chan") * bin_dev, bin_dev)
    onehot = (local_sets[:, None] == set_ids[None, :]).astype(jnp.bfloat16)
    return complex_terms(lax.all_gather(weights, "chan", axis=3, tiled=True), local_spec, onehot)


def solution(mesh):
    in_specs = (P("chan", "beam"), P(None, None, "beam", "chan"), P())
    out_specs = P("chan", None, "beam")
    return jax.shard_map(shards, mesh=mesh, in_specs=in_specs, out_specs=out_specs, check_vma=False)
```

profile of v0, /device:TPU:0, one launch (start us, length us, event | category | flops | bytes accessed | tf_op | source)
XLA Modules:
  0.0 104.1 jit_solution(7308417566398005931)
XLA Ops:
  6.5 4.2 %all-to-all-start = ((bf16[4,64,2048]{2,1,0:T(8,128)(2,1)}), bf16[4,64,2048]{2,1,0:T(8,128)(2,1)S(1)}, u32[]{:S(2)}, u32[]{:S(2)}) async-start(bf16[4,64,2048]{2,1,0:T(8,128)(2,1)} %bitcast.45), calls=%async_computation | async-start | bytes 2097152 | tf_op jit(solution)/shard_map/all_to_all | solution.py:44
  10.8 0.0 all-gather.2.cloned.1.call-start
  10.8 1.8 %copy.38 = bf16[3,2,128,256]{3,2,0,1:T(8,128)(2,1)} copy(bf16[3,2,128,256]{3,2,1,0:T(8,128)(2,1)} %param.6) | data formatting | bytes 786432 | tf_op args[1]
  12.5 0.0 all-gather.2.cloned.1.call-update
  12.6 12.6 %all-to-all-done = bf16[4,64,2048]{2,1,0:T(8,128)(2,1)S(1)} async-done(((bf16[4,64,2048]{2,1,0:T(8,128)(2,1)}), bf16[4,64,2048]{2,1,0:T(8,128)(2,1)S(1)}, u32[]{:S(2)}, u32[]{:S(2)}) %all-to-all-start) | async-done | bytes 1048608 | tf_op jit(solution)/shard_map/all_to_all | solution.py:44
  25.2 0.1 copy.46
  25.3 0.0 copy-start
  25.3 45.1 %while.16 = (s32[]{:T(128)}, f32[256,2,64]{0,2,1:T(8,128)S(1)}, bf16[64,8192]{1,0:T(8,128)(2,1)S(1)}, s32[]{:T(128)}, s32[]{:T(128)}, /*index=5*/s32[]{:T(128)}, s32[]{:T(128)}) while((s32[]{:T(128)}, f32[256,2,64]{0,2,1:T(8,128)S(1)}, bf16[64,8192]{1,0:T(8,128)(2,1)S(1)}, s32[]{:T(128)}, s32[]{:T(128)}, /*index=5*/s32[]{:T(128)}, ...), condition=%wide.region_1.2_spmd.clone, body=%wide.region_0.1_spmd.clone.sunk | while | flops 36111112 | bytes 1382549 | solution.py:35
  25.4 2.5 %cosine_convert_fusion.2 = (bf16[256,1,512]{2,0,1:T(8,128)(2,1)S(1)}, bf16[256,1,512]{2,0,1:T(8,128)(2,1)S(1)}) fusion(s32[512]{0:T(512)S(1)} %iota_add_fusion.4, s32[256]{0:T(256)S(1)} %iota_add_fusion.5), kind=kLoop, calls=%fused_computation.14.clone.1 | loop fusion | flops 2228224 | bytes 527360 | tf_op jit(solution)/shard_map/convert
  27.8 0.3 convolution_add_fusion.2
  28.2 2.5 %cosine_convert_fusion.2 = (bf16[256,1,512]{2,0,1:T(8,128)(2,1)S(1)}, bf16[256,1,512]{2,0,1:T(8,128)(2,1)S(1)}) fusion(s32[512]{0:T(512)S(1)} %iota_add_fusion.4, s32[256]{0:T(256)S(1)} %iota_add_fusion.5), kind=kLoop, calls=%fused_computation.14.clone.1 | loop fusion | flops 2228224 | bytes 527360 | tf_op jit(solution)/shard_map/convert
  30.7 0.3 convolution_add_fusion.2
  31.0 2.5 %cosine_convert_fusion.2 = (bf16[256,1,512]{2,0,1:T(8,128)(2,1)S(1)}, bf16[256,1,512]{2,0,1:T(8,128)(2,1)S(1)}) fusion(s32[512]{0:T(512)S(1)} %iota_add_fusion.4, s32[256]{0:T(256)S(1)} %iota_add_fusion.5), kind=kLoop, calls=%fused_computation.14.clone.1 | loop fusion | flops 2228224 | bytes 527360 | tf_op jit(solution)/shard_map/convert
  33.5 0.3 convolution_add_fusion.2
  33.8 2.5 %cosine_convert_fusion.2 = (bf16[256,1,512]{2,0,1:T(8,128)(2,1)S(1)}, bf16[256,1,512]{2,0,1:T(8,128)(2,1)S(1)}) fusion(s32[512]{0:T(512)S(1)} %iota_add_fusion.4, s32[256]{0:T(256)S(1)} %iota_add_fusion.5), kind=kLoop, calls=%fused_computation.14.clone.1 | loop fusion | flops 2228224 | bytes 527360 | tf_op jit(solution)/shard_map/convert
  36.3 0.3 convolution_add_fusion.2
  36.6 2.5 %cosine_convert_fusion.2 = (bf16[256,1,512]{2,0,1:T(8,128)(2,1)S(1)}, bf16[256,1,512]{2,0,1:T(8,128)(2,1)S(1)}) fusion(s32[512]{0:T(512)S(1)} %iota_add_fusion.4, s32[256]{0:T(256)S(1)} %iota_add_fusion.5), kind=kLoop, calls=%fused_computation.14.clone.1 | loop fusion | flops 2228224 | bytes 527360 | tf_op jit(solution)/shard_map/convert
  39.1 0.3 convolution_add_fusion.2
  39.5 2.5 %cosine_convert_fusion.2 = (bf16[256,1,512]{2,0,1:T(8,128)(2,1)S(1)}, bf16[256,1,512]{2,0,1:T(8,128)(2,1)S(1)}) fusion(s32[512]{0:T(512)S(1)} %iota_add_fusion.4, s32[256]{0:T(256)S(1)} %iota_add_fusion.5), kind=kLoop, calls=%fused_computation.14.clone.1 | loop fusion | flops 2228224 | bytes 527360 | tf_op jit(solution)/shard_map/convert
  41.9 0.3 convolution_add_fusion.2
  42.3 2.5 %cosine_convert_fusion.2 = (bf16[256,1,512]{2,0,1:T(8,128)(2,1)S(1)}, bf16[256,1,512]{2,0,1:T(8,128)(2,1)S(1)}) fusion(s32[512]{0:T(512)S(1)} %iota_add_fusion.4, s32[256]{0:T(256)S(1)} %iota_add_fusion.5), kind=kLoop, calls=%fused_computation.14.clone.1 | loop fusion | flops 2228224 | bytes 527360 | tf_op jit(solution)/shard_map/convert
  44.8 0.3 convolution_add_fusion.2
  45.1 2.5 %cosine_convert_fusion.2 = (bf16[256,1,512]{2,0,1:T(8,128)(2,1)S(1)}, bf16[256,1,512]{2,0,1:T(8,128)(2,1)S(1)}) fusion(s32[512]{0:T(512)S(1)} %iota_add_fusion.4, s32[256]{0:T(256)S(1)} %iota_add_fusion.5), kind=kLoop, calls=%fused_computation.14.clone.1 | loop fusion | flops 2228224 | bytes 527360 | tf_op jit(solution)/shard_map/convert
  47.6 0.3 convolution_add_fusion.2
  47.9 2.5 %cosine_convert_fusion.2 = (bf16[256,1,512]{2,0,1:T(8,128)(2,1)S(1)}, bf16[256,1,512]{2,0,1:T(8,128)(2,1)S(1)}) fusion(s32[512]{0:T(512)S(1)} %iota_add_fusion.4, s32[256]{0:T(256)S(1)} %iota_add_fusion.5), kind=kLoop, calls=%fused_computation.14.clone.1 | loop fusion | flops 2228224 | bytes 527360 | tf_op jit(solution)/shard_map/convert
  50.4 0.3 convolution_add_fusion.2
  50.8 2.5 %cosine_convert_fusion.2 = (bf16[256,1,512]{2,0,1:T(8,128)(2,1)S(1)}, bf16[256,1,512]{2,0,1:T(8,128)(2,1)S(1)}) fusion(s32[512]{0:T(512)S(1)} %iota_add_fusion.4, s32[256]{0:T(256)S(1)} %iota_add_fusion.5), kind=kLoop, calls=%fused_computation.14.clone.1 | loop fusion | flops 2228224 | bytes 527360 | tf_op jit(solution)/shard_map/convert
  53.2 0.3 convolution_add_fusion.2
  53.6 2.5 %cosine_convert_fusion.2 = (bf16[256,1,512]{2,0,1:T(8,128)(2,1)S(1)}, bf16[256,1,512]{2,0,1:T(8,128)(2,1)S(1)}) fusion(s32[512]{0:T(512)S(1)} %iota_add_fusion.4, s32[256]{0:T(256)S(1)} %iota_add_fusion.5), kind=kLoop, calls=%fused_computation.14.clone.1 | loop fusion | flops 2228224 | bytes 527360 | tf_op jit(solution)/shard_map/convert
  56.0 0.3 convolution_add_fusion.2
  56.4 2.5 %cosine_convert_fusion.2 = (bf16[256,1,512]{2,0,1:T(8,128)(2,1)S(1)}, bf16[256,1,512]{2,0,1:T(8,128)(2,1)S(1)}) fusion(s32[512]{0:T(512)S(1)} %iota_add_fusion.4, s32[256]{0:T(256)S(1)} %iota_add_fusion.5), kind=kLoop, calls=%fused_computation.14.clone.1 | loop fusion | flops 2228224 | bytes 527360 | tf_op jit(solution)/shard_map/convert
  58.9 0.3 convolution_add_fusion.2
  59.2 2.5 %cosine_convert_fusion.2 = (bf16[256,1,512]{2,0,1:T(8,128)(2,1)S(1)}, bf16[256,1,512]{2,0,1:T(8,128)(2,1)S(1)}) fusion(s32[512]{0:T(512)S(1)} %iota_add_fusion.4, s32[256]{0:T(256)S(1)} %iota_add_fusion.5), kind=kLoop, calls=%fused_computation.14.clone.1 | loop fusion | flops 2228224 | bytes 527360 | tf_op jit(solution)/shard_map/convert
  61.7 0.3 convolution_add_fusion.2
  62.0 2.5 %cosine_convert_fusion.2 = (bf16[256,1,512]{2,0,1:T(8,128)(2,1)S(1)}, bf16[256,1,512]{2,0,1:T(8,128)(2,1)S(1)}) fusion(s32[512]{0:T(512)S(1)} %iota_add_fusion.4, s32[256]{0:T(256)S(1)} %iota_add_fusion.5), kind=kLoop, calls=%fused_computation.14.clone.1 | loop fusion | flops 2228224 | bytes 527360 | tf_op jit(solution)/shard_map/convert
  64.5 0.3 convolution_add_fusion.2
  64.9 2.5 %cosine_convert_fusion.2 = (bf16[256,1,512]{2,0,1:T(8,128)(2,1)S(1)}, bf16[256,1,512]{2,0,1:T(8,128)(2,1)S(1)}) fusion(s32[512]{0:T(512)S(1)} %iota_add_fusion.4, s32[256]{0:T(256)S(1)} %iota_add_fusion.5), kind=kLoop, calls=%fused_computation.14.clone.1 | loop fusion | flops 2228224 | bytes 527360 | tf_op jit(solution)/shard_map/convert
  67.3 0.3 convolution_add_fusion.2
  67.7 2.5 %cosine_convert_fusion.2 = (bf16[256,1,512]{2,0,1:T(8,128)(2,1)S(1)}, bf16[256,1,512]{2,0,1:T(8,128)(2,1)S(1)}) fusion(s32[512]{0:T(512)S(1)} %iota_add_fusion.4, s32[256]{0:T(256)S(1)} %iota_add_fusion.5), kind=kLoop, calls=%fused_computation.14.clone.1 | loop fusion | flops 2228224 | bytes 527360 | tf_op jit(solution)/shard_map/convert
  70.1 0.3 convolution_add_fusion.2
  70.5 0.1 copy.34
  70.6 5.8 %all_gather.6 = bf16[256,2,256]{0,1,2:T(2,128)(2,1)S(1)} all-gather(bf16[256,2,64]{0,1,2:T(2,128)(2,1)S(1)} %copy.34), channel_id=1, replica_groups=mesh['chan'=8,'beam'=4] {'beam'}, dimensions={2}, use_global_device_ids=true | all-gather | bytes 327680 | tf_op jit(solution)/shard_map/all_gather | solution.py:47
  76.3 1.1 %copy.35 = bf16[256,2,256]{2,1,0:T(2,128)(2,1)} copy(bf16[256,2,256]{0,1,2:T(2,128)(2,1)S(1)} %all_gather.6) | data formatting | bytes 524288 | tf_op jit(solution)/shard_map/all_gather | solution.py:47
  77.5 6.6 %all-to-all-start.1 = ((bf16[256,2,256]{2,1,0:T(2,128)(2,1)}), bf16[256,2,256]{2,1,0:T(2,128)(2,1)S(1)}, u32[]{:S(2)}, u32[]{:S(2)}) async-start(bf16[256,2,256]{2,1,0:T(2,128)(2,1)} %copy.35), calls=%async_computation.1 | async-start | bytes 524288 | tf_op jit(solution)/shard_map/all_to_all | solution.py:50
  84.0 0.0 copy-done
  84.0 0.1 dynamic_slice.13
  84.1 9.3 %all-to-all-done.1 = bf16[256,2,256]{2,1,0:T(2,128)(2,1)S(1)} async-done(((bf16[256,2,256]{2,1,0:T(2,128)(2,1)}), bf16[256,2,256]{2,1,0:T(2,128)(2,1)S(1)}, u32[]{:S(2)}, u32[]{:S(2)}) %all-to-all-start.1) | async-done | bytes 262176 | tf_op jit(solution)/shard_map/all_to_all | solution.py:50
  93.5 0.0 all-gather.2.cloned.1.call-done
  93.6 3.0 %fusion.14 = f32[32,2,2,128]{3,0,1,2:T(8,128)S(1)} fusion(bf16[3,2,128,2048]{3,2,0,1:T(8,128)(2,1)} %all-gather.2.cloned.1.call-done, bf16[32,2,2048]{2,0,1:T(8,128)(2,1)S(1)} %bitcast.44, bf16[32,3]{0,1:T(4,128)(2,1)S(1)} %fusion.24), kind=kOutput, calls=%fused_computation.23 | convolution fusion | flops 202899456 | bytes 3473600 | tf_op jit(solution)/shard_map/gpbc,fgqc->fpqb/dot_general | solution.py:11
  96.6 0.6 copy.41
  (40 shorter events, 0.2 us)
Async XLA Ops:
  6.5 18.7 %all-to-all-start = ((bf16[4,64,2048]{2,1,0:T(8,128)(2,1)}), bf16[4,64,2048]{2,1,0:T(8,128)(2,1)S(1)}, u32[]{:S(2)}, u32[]{:S(2)}) async-start(bf16[4,64,2048]{2,1,0:T(8,128)(2,1)} %bitcast.45), calls=%async_computation | async-start | bytes 2097152 | tf_op jit(solution)/shard_map/all_to_all | solution.py:44
  10.8 82.8 %all-gather.2.cloned.1.call-start = ((), (), s32[]{:S(2)}) async-start(), calls=%async_computation.2 | async-start | bytes 3538944 | tf_op jit(solution)/shard_map/all_gather | solution.py:53
  25.3 58.7 %copy-start = (s32[256]{0:T(256)S(1)}, s32[256]{0:T(256)}, u32[]{:S(2)}) copy-start(s32[256]{0:T(256)} %param.7) | copy-start | bytes 3076
  77.5 16.0 %all-to-all-start.1 = ((bf16[256,2,256]{2,1,0:T(2,128)(2,1)}), bf16[256,2,256]{2,1,0:T(2,128)(2,1)S(1)}, u32[]{:S(2)}, u32[]{:S(2)}) async-start(bf16[256,2,256]{2,1,0:T(2,128)(2,1)} %copy.35), calls=%async_computation.1 | async-start | bytes 524288 | tf_op jit(solution)/shard_map/all_to_all | solution.py:50
Sparse Core Ops, SparseCore 0:
  13.6 65.2 all-gather.1
where the time goes:
time: 104 us
  other arithmetic  39.5 us (38%)
  waiting for transfers between devices  22 us (21%)
  between operations  13.5 us (13%)
  starting transfers between devices  10.8 us (10%)
  matrix products  7.83 us (8%)
  blocking collectives  5.78 us (6%)
  local copies, waits for them, and re-layouts  3.82 us (4%)
    another operation x16, other arithmetic  39.3 us
    all_to_all x1, waiting for transfers between devices, shards(): lax.all_to_all(signals, 'beam', split_axis=0, concat_axis=1, tiled=True)  12.6 us
    all_to_all x1, waiting for transfers between devices, shards(): lax.all_to_all(spectrum, 'chan', split_axis=0, concat_axis=2, tiled=True)  9.34 us
    all_to_all x1, starting transfers between devices, shards(): lax.all_to_all(spectrum, 'chan', split_axis=0, concat_axis=2, tiled=True)  6.57 us
    all_gather x1, blocking collectives, shards(): spectrum = lax.all_gather(own_spec, 'beam', axis=2, tiled=True)  5.78 us
    dot_general x16, matrix products, add_block(): lax.dot_general(twiddle, piece, (((2,), (1,)), ((), ())), preferred_eleme...  4.86 us
    all_to_all x1, starting transfers between devices, shards(): lax.all_to_all(signals, 'beam', split_axis=0, concat_axis=1, tiled=True)  4.24 us
    dot_general x1, matrix products, complex_terms(): jnp.einsum('gpbc,fgqc->fpqb', weight_block, selected, preferred_element_t...  2.97 us
  transfers between devices with their start and end apart: 3, of which 2 were waited for; matrix products, arithmetic and copies ran while one was open for 46% of the time, Pallas kernels for 0%

commit v1 on v0

v1 whole, which is shorter than its diff:
```python
import functools
import math

import jax
import jax.numpy as jnp
from jax import lax
from jax.experimental import pallas as pl
from jax.experimental.pallas import tpu as pltpu
from jax.sharding import PartitionSpec as P

MESH = pl.DeviceIdType.MESH
LANES = 128
ROWS = 16
NT = (((1,), (1,)), ((), ()))


def cos_sin(phase, period):
    quarter = period // 4
    turn = (phase + quarter // 2) // quarter
    angle = (phase - turn * quarter).astype(jnp.float32) * (2.0 * math.pi / period)
    square = angle * angle
    sine = angle * (1 + square * (-1 / 6 + square * (1 / 120 + square * (-1 / 5040 + square / 362880))))
    cosine = 1 + square * (
        -1 / 2 + square * (1 / 24 + square * (-1 / 720 + square * (1 / 40320 - square / 3628800)))
    )
    turn = turn & 3
    swap = (turn & 1) == 1
    first = jnp.where(swap, sine, cosine)
    second = jnp.where(swap, cosine, sine)
    cos_value = jnp.where((turn == 1) | (turn == 2), -first, first)
    sin_value = jnp.where(turn >= 2, -second, second)
    return cos_value, sin_value


def kernel(
    n_chan, n_beam,
    signals_hbm, weights_hbm, group_ref, out_ref,
    signals, weights, twiddle, part, from_pair, from_far, spectrum, group_rows, formed, arrived,
    load_sem, pair_send, pair_recv, far_send, far_recv, spec_send, spec_recv, form_send, form_recv,
):
    chan, beam = lax.axis_index("chan"), lax.axis_index("beam")
    core = lax.rem(beam, 2)
    far_count = n_beam // 2 - 1
    partner = beam + 1 - 2 * core
    fars = [lax.rem(beam + 2 * (s + 1), n_beam) for s in range(far_count)]
    chans = [lax.rem(chan + s + 1, n_chan) for s in range(n_chan - 1)]

    barrier = pltpu.get_barrier_semaphore()
    for other in [partner] + fars:
        pl.semaphore_signal(barrier, inc=1, device_id={"beam": other}, device_id_type=MESH)
    for other in chans:
        pl.semaphore_signal(barrier, inc=1, device_id={"chan": other}, device_id_type=MESH)

    load_signals = pltpu.make_async_copy(signals_hbm, signals, load_sem.at[0])
    load_weights = pltpu.make_async_copy(weights_hbm, weights, load_sem.at[1])
    load_signals.start()
    load_weights.start()

    half, samples = part.shape[2], signals.shape[1]
    block = twiddle.shape[1]
    total = samples * n_beam
    bins = half * 2
    bin_dev = bins // n_chan
    chunks = half // bin_dev
    sets, _, beams, channels = weights.shape
    scale = 1.0 / math.sqrt(total)

    def transform(which, wait):
        def one(step, carry):
            first_bin = which * half + step * block

            def rows(row, carry):
                base = pl.multiple_of(row * ROWS, ROWS)
                frequency = first_bin + base + 1 + lax.broadcasted_iota(jnp.int32, (ROWS, LANES), 0)
                lane = lax.broadcasted_iota(jnp.int32, (ROWS, LANES), 1)
                cos_low, sin_low = cos_sin((frequency * lane) & (total - 1), total)
                high = beam * samples + lane * LANES
                cos_high, sin_high = cos_sin((frequency * high) & (total - 1), total)
                for a in range(samples // LANES):
                    ca = jnp.broadcast_to(cos_high[:, a : a + 1], (ROWS, LANES))
                    sa = jnp.broadcast_to(sin_high[:, a : a + 1], (ROWS, LANES))
                    columns = pl.ds(a * LANES, LANES)
                    twiddle[0, pl.ds(base, ROWS), columns] = (ca * cos_low - sa * sin_low).astype(jnp.bfloat16)
                    twiddle[1, pl.ds(base, ROWS), columns] = (-(sa * cos_low + ca * sin_low)).astype(jnp.bfloat16)
                return carry

            lax.fori_loop(0, block // ROWS, rows, 0)
            if wait:
                load_signals.wait()
            summed = lax.dot_general(
                twiddle[...].reshape(2 * block, samples), signals[...], NT, preferred_element_type=jnp.float32
            )
            at = pl.ds(pl.multiple_of(step * block, block), block)
            part[which, 0, at] = summed[:block]
            part[which, 1, at] = summed[block:]
            return carry

        if half == block:
            one(0, 0)
        else:
            lax.fori_loop(0, half // block, one, 0)

    if half != block:
        load_signals.wait()
    transform(1 - core, half == block)

    pl.semaphore_wait(barrier, n_beam // 2 + n_chan - 1)
    to_pair = pltpu.make_async_remote_copy(
        src_ref=part.at[1 - core], dst_ref=from_pair, send_sem=pair_send, recv_sem=pair_recv,
        device_id={"beam": partner}, device_id_type=MESH,
    )
    to_pair.start()
    transform(core, False)

    group = jnp.broadcast_to(group_ref[...].astype(jnp.float32), (LANES, bins))
    group_rows[...] = group.T

    to_pair.wait_recv()

    def order(step):
        return lax.rem(chan + 1 + step, chunks)

    def rows_of(chunk):
        return pl.ds(pl.multiple_of(chunk * bin_dev, bin_dev), bin_dev)

    def far_copy(chunk, s):
        return pltpu.make_async_remote_copy(
            src_ref=part.at[core, :, rows_of(chunk)], dst_ref=from_far.at[s, :, rows_of(chunk)],
            send_sem=far_send.at[s, chunk], recv_sem=far_recv.at[s, chunk],
            device_id={"beam": fars[s]}, device_id_type=MESH,
        )

    def spec_copy(which, chunk):
        return pltpu.make_async_remote_copy(
            src_ref=spectrum.at[which, :, rows_of(chunk)], dst_ref=spectrum.at[which, :, rows_of(chunk)],
            send_sem=spec_send.at[chunk], recv_sem=spec_recv.at[chunk],
            device_id={"beam": partner}, device_id_type=MESH,
        )

    def form_copy(source, target):
        return pltpu.make_async_remote_copy(
            src_ref=formed.at[target], dst_ref=arrived.at[source],
            send_sem=form_send.at[target], recv_sem=form_recv.at[source],
            device_id={"chan": target}, device_id_type=MESH,
        )

    for step in range(chunks):
        chunk = order(step)
        at = rows_of(chunk)
        part[core, :, at] = part[core, :, at] + from_pair[:, at]
        for s in range(far_count):
            far_copy(chunk, s).start()

    load_weights.wait()

    def form(which, chunk):
        at = rows_of(chunk)
        target = which * chunks + chunk
        spec = spectrum[which, :, at].reshape(2 * bin_dev, channels)
        products = lax.dot_general(
            spec, weights[...].reshape(sets * 2 * beams, channels), NT, preferred_element_type=jnp.float32
        )
        ids = group_rows[pl.ds(pl.multiple_of(target * bin_dev, bin_dev), bin_dev), :]
        real = imag = jnp.zeros((bin_dev, beams), jnp.float32)
        for g in range(sets):
            left = slice(2 * g * beams, (2 * g + 1) * beams)
            right = slice((2 * g + 1) * beams, (2 * g + 2) * beams)
            chosen = ids[:, :1] == g
            real = jnp.where(chosen, products[:bin_dev, left] - products[bin_dev:, right], real)
            imag = jnp.where(chosen, products[bin_dev:, left] + products[:bin_dev, right], imag)
        formed[target, 0] = real
        formed[target, 1] = imag

        @pl.when(target != chan)
        def _():
            form_copy(chan, target).start()

    def far_sum(chunk):
        at = rows_of(chunk)
        value = part[core, :, at]
        for s in range(far_count):
            far_copy(chunk, s).wait_recv()
            value = value + from_far[s, :, at]
        spectrum[core, :, at] = (value * scale).astype(jnp.bfloat16)
        spec_copy(core, chunk).start()

    for step in range(chunks):
        chunk = order(step)
        far_sum(chunk)
        form(core, chunk)
        if step:
            before = order(step - 1)
            spec_copy(1 - core, before).wait_recv()
            form(1 - core, before)
    last = order(chunks - 1)
    spec_copy(1 - core, last).wait_recv()
    form(1 - core, last)

    value = formed[chan]
    for other in reversed(chans):
        form_copy(other, other).wait_recv()
        value = value + arrived[other]
    out_ref[...] = value

    to_pair.wait_send()
    for chunk in range(chunks):
        for s in range(far_count):
            far_copy(chunk, s).wait_send()
        spec_copy(core, chunk).wait_send()
    for other in chans:
        form_copy(chan, other).wait_send()


def shards(n_chan, n_beam, signals, weights, bin_group):
    channels, samples = signals.shape
    sets, _, beams, _ = weights.shape
    bins = bin_group.shape[0]
    half, bin_dev = bins // 2, bins // n_chan
    chunks = half // bin_dev
    fars = n_beam // 2 - 1
    block = min(half, 128)
    dma = pltpu.SemaphoreType.DMA
    out = pl.pallas_call(
        functools.partial(kernel, n_chan, n_beam),
        out_shape=jax.ShapeDtypeStruct((2, bin_dev, beams), jnp.float32),
        in_specs=[
            pl.BlockSpec(memory_space=pl.ANY),
            pl.BlockSpec(memory_space=pl.ANY),
            pl.BlockSpec(memory_space=pltpu.VMEM),
        ],
        out_specs=pl.BlockSpec(memory_space=pltpu.VMEM),
        scratch_shapes=[
            pltpu.VMEM(signals.shape, signals.dtype),
            pltpu.VMEM(weights.shape, weights.dtype),
            pltpu.VMEM((2, block, samples), jnp.bfloat16),
            pltpu.VMEM((2, 2, half, channels), jnp.float32),
            pltpu.VMEM((2, half, channels), jnp.float32),
            pltpu.VMEM((fars, 2, half, channels), jnp.float32),
            pltpu.VMEM((2, 2, half, channels), jnp.bfloat16),
            pltpu.VMEM((bins, LANES), jnp.float32),
            pltpu.VMEM((n_chan, 2, bin_dev, beams), jnp.float32),
            pltpu.VMEM((n_chan, 2, bin_dev, beams), jnp.float32),
            dma((2,)), dma, dma, dma((fars, chunks)), dma((fars, chunks)),
            dma((chunks,)), dma((chunks,)), dma((n_chan,)), dma((n_chan,)),
        ],
        compiler_params=pltpu.CompilerParams(
            collective_id=0, has_side_effects=True, vmem_limit_bytes=60 * 1024 * 1024
        ),
        name="beamform",
    )(signals, weights, bin_group.reshape(1, bins))
    return jnp.swapaxes(out, 0, 1)


def solution(mesh):
    in_specs = (P("chan", "beam"), P(None, None, "beam", "chan"), P())
    out_specs = P("chan", None, "beam")
    body = functools.partial(shards, mesh.shape["chan"], mesh.shape["beam"])
    return jax.shard_map(body, mesh=mesh, in_specs=in_specs, out_specs=out_specs, check_vma=False)
```

time: 104 us -> 24.2 us (0.23)
  other arithmetic: 39.5 us -> 0 us
  Pallas kernels: 0 us -> 22.6 us
  waiting for transfers between devices: 22 us -> 0 us
  between operations: 13.5 us -> 0.01 us
  starting transfers between devices: 10.8 us -> 0 us
  matrix products: 7.83 us -> 0 us
  blocking collectives: 5.78 us -> 0 us
  local copies, waits for them, and re-layouts: 3.82 us -> 1.4 us
    another operation x17 -> x0, other arithmetic: 39.3 us -> none
    pallas_call x0 -> x1, Pallas kernels: none -> 22.6 us  [shards(): pl.pallas_call(functools.partial(kernel, n_chan, n_beam), out_shape=jax.S...]
    all_to_all x2 -> x0, waiting for transfers between devices: 22 us -> none  [the longest x1 12.6 us: shards(): lax.all_to_all(signals, 'beam', split_axis=0, concat_axis=1, tiled=True)]
    all_to_all x2 -> x0, starting transfers between devices: 10.8 us -> none  [the longest x1 6.57 us: shards(): lax.all_to_all(spectrum, 'chan', split_axis=0, concat_axis=2, tiled=True)]
    dot_general x17 -> x0, matrix products: 7.83 us -> none  [the longest x16 4.86 us: add_block(): lax.dot_general(twiddle, piece, (((2,), (1,)), ((), ())), preferred_eleme...]
    all_gather x1 -> x0, blocking collectives: 5.78 us -> none  [shards(): spectrum = lax.all_gather(own_spec, 'beam', axis=2, tiled=True)]
    unnamed x3 -> x0, local copies, waits for them, and re-layouts: 1.77 us -> none
    transpose x0 -> x1, local copies, waits for them, and re-layouts: none -> 1.4 us  [shards(): return jnp.swapaxes(out, 0, 1)]
  transfers between devices with their start and end apart: 3 -> 0, of which waited for: 2 -> 0; matrix products, arithmetic and copies ran while one was open for 46% -> 0% of each run, Pallas kernels for 0% -> 0%
where the time goes in v1:
time: 24.2 us; the launch traced here: 24 us
  Pallas kernels  22.6 us (93%)
  local copies, waits for them, and re-layouts  1.4 us (6%)
    pallas_call x1, Pallas kernels, shards(): pl.pallas_call(functools.partial(kernel, n_chan, n_beam), out_shape=jax.S...  22.6 us
    transpose x1, local copies, waits for them, and re-layouts, shards(): return jnp.swapaxes(out, 0, 1)  1.4 us

profile of v1, /device:TPU:0, one launch (start us, length us, event | category | flops | bytes accessed | tf_op | source)
XLA Modules:
  0.0 24.0 jit_solution(4759226443714123619)
XLA Ops:
  0.0 22.6 %beamform.1 = f32[2,32,128]{2,1,0:T(8,128)} custom-call(bf16[256,2048]{1,0:T(8,128)(2,1)} %signals_hbm.1, bf16[3,2,128,256]{3,2,1,0:T(8,128)(2,1)} %weights_hbm.1, s32[1,256]{1,0:T(1,128)} %bitcast.3), custom_call_target="tpu_custom_call" | custom-call | tf_op jit(solution)/shard_map/beamform/pallas_call | solution.py:223
  22.6 1.4 %copy.4 = f32[32,2,128]{2,1,0:T(2,128)} copy(f32[32,2,128]{2,0,1:T(8,128)} %bitcast.2) | data formatting | bytes 65536 | tf_op jit(solution)/shard_map/transpose | solution.py:251

commit v2 on v0

v2 whole, which is shorter than its diff:
```python
import functools
import math

import jax
import jax.numpy as jnp
from jax import lax
from jax.experimental import pallas as pl
from jax.experimental.pallas import tpu as pltpu
from jax.sharding import PartitionSpec as P

MESH = pl.DeviceIdType.MESH
LANES = 128
ROWS = 16
STREAMS = 4
SENT = jnp.float32
NT = (((1,), (1,)), ((), ()))


def cos_sin(phase, period):
    quarter = period // 4
    turn = (phase + quarter // 2) >> (quarter.bit_length() - 1)
    angle = (phase - turn * quarter).astype(jnp.float32) * (2.0 * math.pi / period)
    square = angle * angle
    sine = angle * (1 + square * (-1 / 6 + square * (1 / 120 + square * (-1 / 5040 + square / 362880))))
    cosine = 1 + square * (
        -1 / 2 + square * (1 / 24 + square * (-1 / 720 + square * (1 / 40320 - square / 3628800)))
    )
    turn = turn & 3
    swap = (turn & 1) == 1
    first = jnp.where(swap, sine, cosine)
    second = jnp.where(swap, cosine, sine)
    cos_value = jnp.where((turn == 1) | (turn == 2), -first, first)
    sin_value = jnp.where(turn >= 2, -second, second)
    return cos_value, sin_value


def flip(index, mask, count):
    if count & (count - 1):
        return lax.rem(index + mask, count)
    result, weight = 0, 1
    while weight < count:
        result = result + (index // weight + mask // weight) % 2 * weight
        weight *= 2
    return result


def loop(count, body):
    if count <= 8:
        for step in range(count):
            body(step)
    else:
        lax.fori_loop(0, count, lambda step, carry: (body(step), carry)[1], 0)


def kernel(
    n_chan, n_beam,
    signals_hbm, weights_hbm, group_ref, out_ref,
    signals, weights, twiddle, part, from_pair, from_far, spectrum, group_rows, formed, arrived,
    load_sem, pair_send, pair_recv, far_send, far_recv, spec_send, spec_recv, form_send, form_recv,
):
    chan, beam = lax.axis_index("chan"), lax.axis_index("beam")
    core = lax.rem(beam, 2)
    far_count = n_beam // 2 - 1
    partner = beam + 1 - 2 * core
    fars = [lax.rem(beam + 2 * (s + 1), n_beam) for s in range(far_count)]

    barrier = pltpu.get_barrier_semaphore()
    for other in [partner] + fars:
        pl.semaphore_signal(barrier, inc=1, device_id={"beam": other}, device_id_type=MESH)

    def greet(step):
        other = flip(chan, n_chan - 1 - step, n_chan)
        pl.semaphore_signal(barrier, inc=1, device_id={"chan": other}, device_id_type=MESH)

    loop(n_chan - 1, greet)

    load_signals = pltpu.make_async_copy(signals_hbm, signals, load_sem.at[0])
    load_weights = pltpu.make_async_copy(weights_hbm, weights, load_sem.at[1])
    load_signals.start()
    load_weights.start()

    bins, samples = part.shape[1], signals.shape[1]
    block = twiddle.shape[1]
    blocks = bins // block
    total = samples * n_beam
    bin_dev = bins // n_chan
    per_block = block // bin_dev
    sets, _, beams, channels = weights.shape
    scale = 1.0 / math.sqrt(total)

    def block_at(step):
        return pl.multiple_of(flip(chan // per_block, blocks - 1 - step, blocks) * block, block)

    def target_of(step):
        return flip(chan, n_chan - 1 - step, n_chan)

    def rows_of(target):
        return pl.ds(pl.multiple_of(target * bin_dev, bin_dev), bin_dev)

    def make_twiddle(start):
        def rows(row, carry):
            base = pl.multiple_of(row * ROWS, ROWS)
            frequency = start + base + 1 + lax.broadcasted_iota(jnp.int32, (ROWS, LANES), 0)
            lane = lax.broadcasted_iota(jnp.int32, (ROWS, LANES), 1)
            cosine, sine = cos_sin((frequency * (beam * samples + lane)) & (total - 1), total)
            stride = STREAMS * LANES
            turns = [(cosine, sine)]
            cos_one, sin_one = cos_sin((frequency * LANES) & (total - 1), total)
            cos_turn, sin_turn = cos_one, sin_one
            doubled = 1
            while doubled < STREAMS:
                turns += [(c * cos_turn - s * sin_turn, s * cos_turn + c * sin_turn) for c, s in turns]
                cos_turn, sin_turn = cos_turn * cos_turn - sin_turn * sin_turn, 2 * cos_turn * sin_turn
                doubled *= 2
            for a in range(0, samples, stride):
                for b, (c, s) in enumerate(turns):
                    at = pl.ds(base, ROWS), pl.ds(a + b * LANES, LANES)
                    twiddle[0, at[0], at[1]] = c.astype(jnp.bfloat16)
                    twiddle[1, at[0], at[1]] = (-s).astype(jnp.bfloat16)
                turns = [(c * cos_turn - s * sin_turn, s * cos_turn + c * sin_turn) for c, s in turns]
            return carry

        lax.fori_loop(0, block // ROWS, rows, 0)

    def transform(kind, start):
        part[kind, pl.ds(start, block)] = lax.dot_general(
            twiddle[kind], signals[...], NT, preferred_element_type=jnp.float32
        )

    def pair_copy(step):
        at = pl.ds(block_at(step), block)
        return pltpu.make_async_remote_copy(
            src_ref=part.at[1 - core, at], dst_ref=from_pair.at[at],
            send_sem=pair_send.at[step], recv_sem=pair_recv.at[step],
            device_id={"beam": partner}, device_id_type=MESH,
        )

    def far_copy(step, s):
        at = rows_of(target_of(step))
        return pltpu.make_async_remote_copy(
            src_ref=part.at[core, at], dst_ref=from_far.at[s, at],
            send_sem=far_send.at[s, step], recv_sem=far_recv.at[s, step],
            device_id={"beam": fars[s]}, device_id_type=MESH,
        )

    def spec_copy(kind, step):
        at = rows_of(target_of(step))
        return pltpu.make_async_remote_copy(
            src_ref=spectrum.at[kind, at], dst_ref=spectrum.at[kind, at],
            send_sem=spec_send.at[step], recv_sem=spec_recv.at[step],
            device_id={"beam": partner}, device_id_type=MESH,
        )

    def form_copy(step):
        target = target_of(step)
        return pltpu.make_async_remote_copy(
            src_ref=formed.at[step], dst_ref=arrived.at[step],
            send_sem=form_send.at[step], recv_sem=form_recv.at[step],
            device_id={"chan": target}, device_id_type=MESH,
        )

    def pair_sum(step):
        pair_copy(step).wait_recv()
        for inner in range(per_block):
            chunk = step * per_block + inner
            at = rows_of(target_of(chunk))
            part[core, at] = part[core, at] + from_pair[at]
            for s in range(far_count):
                far_copy(chunk, s).start()

    make_twiddle(block_at(0))
    load_signals.wait()
    transform(1 - core, block_at(0))
    pl.semaphore_wait(barrier, n_beam // 2 + n_chan - 1)
    pair_copy(0).start()
    transform(core, block_at(0))

    def one_block(before):
        start = block_at(before + 1)
        make_twiddle(start)
        pair_sum(before)
        transform(1 - core, start)
        pair_copy(before + 1).start()
        transform(core, start)

    loop(blocks - 1, one_block)
    pair_sum(blocks - 1)

    group = jnp.broadcast_to(group_ref[...].astype(jnp.float32), (LANES, bins))
    group_rows[...] = group.T
    load_weights.wait()

    def far_sum(step):
        at = rows_of(target_of(step))
        value = part[core, at]
        for s in range(far_count):
            far_copy(step, s).wait_recv()
            value = value + from_far[s, at]
        spectrum[core, at] = (value * scale).astype(jnp.bfloat16)
        spec_copy(core, step).start()

    def form(step):
        at = rows_of(target_of(step))
        spec_copy(1 - core, step).wait_recv()
        products = lax.dot_general(
            spectrum[:, at].reshape(2 * bin_dev, channels),
            weights[...].reshape(sets * 2 * beams, channels), NT, preferred_element_type=jnp.float32,
        )
        ids = group_rows[at, :][:, :1]
        real = imag = jnp.zeros((bin_dev, beams), jnp.float32)
        for g in range(sets):
            left = slice(2 * g * beams, (2 * g + 1) * beams)
            right = slice((2 * g + 1) * beams, (2 * g + 2) * beams)
            real = jnp.where(ids == g, products[:bin_dev, left] - products[bin_dev:, right], real)
            imag = jnp.where(ids == g, products[bin_dev:, left] + products[:bin_dev, right], imag)
        return real, imag

    def send_formed(step):
        real, imag = form(step)
        formed[step, 0] = real.astype(formed.dtype)
        formed[step, 1] = imag.astype(formed.dtype)
        form_copy(step).start()

    def one_chunk(before):
        far_sum(before + 1)
        send_formed(before)

    far_sum(0)
    loop(n_chan - 1, one_chunk)
    real, imag = form(n_chan - 1)
    out_ref[:, 0, :] = real
    out_ref[:, 1, :] = imag

    def collect(step):
        form_copy(step).wait_recv()
        out_ref[:, 0, :] = out_ref[:, 0, :] + arrived[step, 0].astype(jnp.float32)
        out_ref[:, 1, :] = out_ref[:, 1, :] + arrived[step, 1].astype(jnp.float32)

    if n_chan <= 8:
        for step in range(n_chan - 1):
            form_copy(step).wait_recv()
            real = real + arrived[step, 0].astype(jnp.float32)
            imag = imag + arrived[step, 1].astype(jnp.float32)
        out_ref[:, 0, :] = real
        out_ref[:, 1, :] = imag
    else:
        loop(n_chan - 1, collect)

    loop(blocks, lambda step: pair_copy(step).wait_send())
    for s in range(far_count):
        loop(n_chan, lambda step: far_copy(step, s).wait_send())
    loop(n_chan, lambda step: spec_copy(core, step).wait_send())
    loop(n_chan - 1, lambda step: form_copy(step).wait_send())


def shards(n_chan, n_beam, signals, weights, bin_group):
    channels, samples = signals.shape
    sets, _, beams, _ = weights.shape
    bins = bin_group.shape[0]
    bin_dev = bins // n_chan
    fars = n_beam // 2 - 1
    block = min(bins, max(256, bin_dev))
    blocks = bins // block
    dma = pltpu.SemaphoreType.DMA
    return pl.pallas_call(
        functools.partial(kernel, n_chan, n_beam),
        out_shape=jax.ShapeDtypeStruct((bin_dev, 2, beams), jnp.float32),
        in_specs=[
            pl.BlockSpec(memory_space=pl.ANY),
            pl.BlockSpec(memory_space=pl.ANY),
            pl.BlockSpec(memory_space=pltpu.VMEM),
        ],
        out_specs=pl.BlockSpec(memory_space=pltpu.VMEM),
        scratch_shapes=[
            pltpu.VMEM(signals.shape, signals.dtype),
            pltpu.VMEM(weights.shape, weights.dtype),
            pltpu.VMEM((2, block, samples), jnp.bfloat16),
            pltpu.VMEM((2, bins, channels), jnp.float32),
            pltpu.VMEM((bins, channels), jnp.float32),
            pltpu.VMEM((fars, bins, channels), jnp.float32),
            pltpu.VMEM((2, bins, channels), jnp.bfloat16),
            pltpu.VMEM((bins, LANES), jnp.float32),
            pltpu.VMEM((n_chan, 2, bin_dev, beams), SENT),
            pltpu.VMEM((n_chan, 2, bin_dev, beams), SENT),
            dma((2,)), dma((blocks,)), dma((blocks,)), dma((fars, n_chan)), dma((fars, n_chan)),
            dma((n_chan,)), dma((n_chan,)), dma((n_chan,)), dma((n_chan,)),
        ],
        compiler_params=pltpu.CompilerParams(
            collective_id=0, has_side_effects=True, vmem_limit_bytes=60 * 1024 * 1024
        ),
        name="beamform",
    )(signals, weights, bin_group.reshape(1, bins))


def solution(mesh):
    in_specs = (P("chan", "beam"), P(None, None, "beam", "chan"), P())
    out_specs = P("chan", None, "beam")
    body = functools.partial(shards, mesh.shape["chan"], mesh.shape["beam"])
    return jax.shard_map(body, mesh=mesh, in_specs=in_specs, out_specs=out_specs, check_vma=False)
```

time: 104 us -> 22.5 us (0.22)
  other arithmetic: 39.5 us -> 0 us
  waiting for transfers between devices: 22 us -> 0 us
  Pallas kernels: 0 us -> 20.9 us
  between operations: 13.5 us -> 0.01 us
  starting transfers between devices: 10.8 us -> 0 us
  matrix products: 7.83 us -> 0 us
  blocking collectives: 5.78 us -> 0 us
  local copies, waits for them, and re-layouts: 3.82 us -> 1.38 us
    another operation x17 -> x0, other arithmetic: 39.3 us -> none
    all_to_all x2 -> x0, waiting for transfers between devices: 22 us -> none  [the longest x1 12.6 us: shards(): lax.all_to_all(signals, 'beam', split_axis=0, concat_axis=1, tiled=True)]
    pallas_call x0 -> x1, Pallas kernels: none -> 20.9 us  [shards(): pl.pallas_call(functools.partial(kernel, n_chan, n_beam), out_shape=jax.S...]
    all_to_all x2 -> x0, starting transfers between devices: 10.8 us -> none  [the longest x1 6.57 us: shards(): lax.all_to_all(spectrum, 'chan', split_axis=0, concat_axis=2, tiled=True)]
    dot_general x17 -> x0, matrix products: 7.83 us -> none  [the longest x16 4.86 us: add_block(): lax.dot_general(twiddle, piece, (((2,), (1,)), ((), ())), preferred_eleme...]
    all_gather x1 -> x0, blocking collectives: 5.78 us -> none  [shards(): spectrum = lax.all_gather(own_spec, 'beam', axis=2, tiled=True)]
    all_gather x1 -> x0, local copies, waits for them, and re-layouts: 1.12 us -> none  [shards(): spectrum = lax.all_gather(own_spec, 'beam', axis=2, tiled=True)]
  transfers between devices with their start and end apart: 3 -> 0, of which waited for: 2 -> 0; matrix products, arithmetic and copies ran while one was open for 46% -> 0% of each run, Pallas kernels for 0% -> 0%
where the time goes in v2:
time: 22.5 us; the launch traced here: 22.3 us
  Pallas kernels  20.9 us (93%)
  local copies, waits for them, and re-layouts  1.38 us (6%)
    pallas_call x1, Pallas kernels, shards(): pl.pallas_call(functools.partial(kernel, n_chan, n_beam), out_shape=jax.S...  20.9 us
    unnamed x1, local copies, waits for them, and re-layouts  1.38 us

profile of v2, /device:TPU:0, one launch (start us, length us, event | category | flops | bytes accessed | tf_op | source)
XLA Modules:
  0.0 22.3 jit_solution(6258357164845529861)
XLA Ops:
  0.0 20.9 %beamform.1 = f32[32,2,128]{2,1,0:T(2,128)} custom-call(bf16[256,2048]{1,0:T(8,128)(2,1)} %signals_hbm.1, bf16[3,2,128,256]{3,2,1,0:T(8,128)(2,1)} %weights_hbm.1, s32[1,256]{1,0:T(1,128)} %bitcast.1), custom_call_target="tpu_custom_call" | custom-call | tf_op jit(solution)/shard_map/beamform/pallas_call | solution.py:265
  20.9 1.4 %copy.5 = f32[32,2,128]{2,1,0:T(2,128)} copy(f32[32,2,128]{2,1,0:T(2,128)} %beamform.1) | data formatting | bytes 65536

commit v3 on v2

--- a/solution.py
+++ b/solution.py
@@ -12,7 +12,8 @@
 LANES = 128
 ROWS = 16
 STREAMS = 4
-SENT = jnp.float32
+PIECES = 4
+SENT = jnp.bfloat16
 NT = (((1,), (1,)), ((), ()))
 
 
@@ -128,7 +129,9 @@
         )
 
     def pair_copy(step):
-        at = pl.ds(block_at(step), block)
+        size = block // PIECES
+        inner = flip(chan % per_block // (per_block // PIECES), PIECES - 1 - step % PIECES, PIECES)
+        at = pl.ds(pl.multiple_of(block_at(step // PIECES) + inner * size, size), size)
         return pltpu.make_async_remote_copy(
             src_ref=part.at[1 - core, at], dst_ref=from_pair.at[at],
             send_sem=pair_send.at[step], recv_sem=pair_recv.at[step],
@@ -160,8 +163,9 @@
         )
 
     def pair_sum(step):
-        pair_copy(step).wait_recv()
         for inner in range(per_block):
+            if inner % (per_block // PIECES) == 0:
+                pair_copy(step * PIECES + inner // (per_block // PIECES)).wait_recv()
             chunk = step * per_block + inner
             at = rows_of(target_of(chunk))
             part[core, at] = part[core, at] + from_pair[at]
@@ -172,7 +176,8 @@
     load_signals.wait()
     transform(1 - core, block_at(0))
     pl.semaphore_wait(barrier, n_beam // 2 + n_chan - 1)
-    pair_copy(0).start()
+    for piece in range(PIECES):
+        pair_copy(piece).start()
     transform(core, block_at(0))
 
     def one_block(before):
@@ -180,7 +185,8 @@
         make_twiddle(start)
         pair_sum(before)
         transform(1 - core, start)
-        pair_copy(before + 1).start()
+        for piece in range(PIECES):
+            pair_copy((before + 1) * PIECES + piece).start()
         transform(core, start)
 
     loop(blocks - 1, one_block)
@@ -228,25 +234,21 @@
     far_sum(0)
     loop(n_chan - 1, one_chunk)
     real, imag = form(n_chan - 1)
-    out_ref[:, 0, :] = real
-    out_ref[:, 1, :] = imag
-
-    def collect(step):
+    real_rows, imag_rows = pl.ds(0, bin_dev, stride=2), pl.ds(1, bin_dev, stride=2)
+
+    def collect(step, value):
         form_copy(step).wait_recv()
-        out_ref[:, 0, :] = out_ref[:, 0, :] + arrived[step, 0].astype(jnp.float32)
-        out_ref[:, 1, :] = out_ref[:, 1, :] + arrived[step, 1].astype(jnp.float32)
+        return value[0] + arrived[step, 0].astype(jnp.float32), value[1] + arrived[step, 1].astype(jnp.float32)
 
     if n_chan <= 8:
         for step in range(n_chan - 1):
-            form_copy(step).wait_recv()
-            real = real + arrived[step, 0].astype(jnp.float32)
-            imag = imag + arrived[step, 1].astype(jnp.float32)
-        out_ref[:, 0, :] = real
-        out_ref[:, 1, :] = imag
+            real, imag = collect(step, (real, imag))
     else:
-        loop(n_chan - 1, collect)
-
-    loop(blocks, lambda step: pair_copy(step).wait_send())
+        real, imag = lax.fori_loop(0, n_chan - 1, collect, (real, imag))
+    out_ref[real_rows, :] = real
+    out_ref[imag_rows, :] = imag
+
+    loop(blocks * PIECES, lambda step: pair_copy(step).wait_send())
     for s in range(far_count):
         loop(n_chan, lambda step: far_copy(step, s).wait_send())
     loop(n_chan, lambda step: spec_copy(core, step).wait_send())
@@ -264,7 +266,7 @@
     dma = pltpu.SemaphoreType.DMA
     return pl.pallas_call(
         functools.partial(kernel, n_chan, n_beam),
-        out_shape=jax.ShapeDtypeStruct((bin_dev, 2, beams), jnp.float32),
+        out_shape=jax.ShapeDtypeStruct((2 * bin_dev, beams), jnp.float32),
         in_specs=[
             pl.BlockSpec(memory_space=pl.ANY),
             pl.BlockSpec(memory_space=pl.ANY),
@@ -282,14 +284,14 @@
             pltpu.VMEM((bins, LANES), jnp.float32),
             pltpu.VMEM((n_chan, 2, bin_dev, beams), SENT),
             pltpu.VMEM((n_chan, 2, bin_dev, beams), SENT),
-            dma((2,)), dma((blocks,)), dma((blocks,)), dma((fars, n_chan)), dma((fars, n_chan)),
+            dma((2,)), dma((blocks * PIECES,)), dma((blocks * PIECES,)), dma((fars, n_chan)), dma((fars, n_chan)),
             dma((n_chan,)), dma((n_chan,)), dma((n_chan,)), dma((n_chan,)),
         ],
         compiler_params=pltpu.CompilerParams(
             collective_id=0, has_side_effects=True, vmem_limit_bytes=60 * 1024 * 1024
         ),
         name="beamform",
-    )(signals, weights, bin_group.reshape(1, bins))
+    )(signals, weights, bin_group.reshape(1, bins)).reshape(bin_dev, 2, beams)
 
 
 def solution(mesh):

time: 22.5 us -> 21.4 us (0.951)
  Pallas kernels: 20.9 us -> 19.8 us
    pallas_call x1, Pallas kernels: 20.9 us -> 19.8 us  [shards(): pl.pallas_call(functools.partial(kernel, n_chan, n_beam), out_shape=jax.S...]
where the time goes in v3:
time: 21.4 us; the launch traced here: 21.2 us
  Pallas kernels  19.8 us (93%)
  local copies, waits for them, and re-layouts  1.38 us (6%)
    pallas_call x1, Pallas kernels, shards(): pl.pallas_call(functools.partial(kernel, n_chan, n_beam), out_shape=jax.S...  19.8 us
    unnamed x1, local copies, waits for them, and re-layouts  1.38 us

profile of v3, /device:TPU:0, one launch (start us, length us, event | category | flops | bytes accessed | tf_op | source)
XLA Modules:
  0.0 21.2 jit_solution(15352234134467887812)
XLA Ops:
  0.0 19.8 %beamform.1 = f32[64,128]{1,0:T(8,128)} custom-call(bf16[256,2048]{1,0:T(8,128)(2,1)} %signals_hbm.1, bf16[3,2,128,256]{3,2,1,0:T(8,128)(2,1)} %weights_hbm.1, s32[1,256]{1,0:T(1,128)} %bitcast.3), custom_call_target="tpu_custom_call" | custom-call | tf_op jit(solution)/shard_map/beamform/pallas_call | solution.py:267
  19.9 1.4 %copy.5 = f32[32,2,128]{2,1,0:T(2,128)} copy(f32[32,2,128]{2,1,0:T(2,128)} %bitcast.2) | data formatting | bytes 65536

commit v4 on v3

--- a/solution.py
+++ b/solution.py
@@ -233,18 +233,26 @@
 
     far_sum(0)
     loop(n_chan - 1, one_chunk)
-    real, imag = form(n_chan - 1)
     real_rows, imag_rows = pl.ds(0, bin_dev, stride=2), pl.ds(1, bin_dev, stride=2)
 
     def collect(step, value):
         form_copy(step).wait_recv()
         return value[0] + arrived[step, 0].astype(jnp.float32), value[1] + arrived[step, 1].astype(jnp.float32)
 
+    early = n_chan // 2
+    value = (jnp.zeros((bin_dev, beams), jnp.float32),) * 2
     if n_chan <= 8:
-        for step in range(n_chan - 1):
+        for step in range(early):
+            value = collect(step, value)
+    else:
+        value = lax.fori_loop(0, early, collect, value)
+    real, imag = form(n_chan - 1)
+    real, imag = real + value[0], imag + value[1]
+    if n_chan <= 8:
+        for step in range(early, n_chan - 1):
             real, imag = collect(step, (real, imag))
     else:
-        real, imag = lax.fori_loop(0, n_chan - 1, collect, (real, imag))
+        real, imag = lax.fori_loop(early, n_chan - 1, collect, (real, imag))
     out_ref[real_rows, :] = real
     out_ref[imag_rows, :] = imag
 

time: 21.4 us -> 21.4 us (level)
  no operation moved by 1% of the time
where the time goes in v4:
time: 21.4 us; the launch traced here: 21.2 us
  Pallas kernels  19.8 us (93%)
  local copies, waits for them, and re-layouts  1.38 us (6%)
    pallas_call x1, Pallas kernels, shards(): pl.pallas_call(functools.partial(kernel, n_chan, n_beam), out_shape=jax.S...  19.8 us
    unnamed x1, local copies, waits for them, and re-layouts  1.38 us

profile of v4, /device:TPU:0, one launch (start us, length us, event | category | flops | bytes accessed | tf_op | source)
XLA Modules:
  0.0 21.2 jit_solution(12260296778142673479)
XLA Ops:
  0.0 19.8 %beamform.1 = f32[64,128]{1,0:T(8,128)} custom-call(bf16[256,2048]{1,0:T(8,128)(2,1)} %signals_hbm.1, bf16[3,2,128,256]{3,2,1,0:T(8,128)(2,1)} %weights_hbm.1, s32[1,256]{1,0:T(1,128)} %bitcast.3), custom_call_target="tpu_custom_call" | custom-call | tf_op jit(solution)/shard_map/beamform/pallas_call | solution.py:275
  19.9 1.4 %copy.5 = f32[32,2,128]{2,1,0:T(2,128)} copy(f32[32,2,128]{2,1,0:T(2,128)} %bitcast.2) | data formatting | bytes 65536
